TPU v7x, 32 devices: a whole 2x2x4 slice. The times are simulated.
32 devices in a mesh: gx: 2 (over x), gy: 4 (over y, core), gz: 4 (over z).
Axes of the slice: x: 2, y: 2, z: 4, core: 2. Of those that a mesh axis runs over, the one named last changes fastest.
Arguments:
- blocks: bfloat16 [512, 128, 1024], P(('gx', 'gy', 'gz')), may hold values from -0.375 to 0.375
- counts: int32 [512], P(('gx', 'gy', 'gz')), may hold values from 1 to 128
- owner: int32 [512, 1], P(('gx', 'gy', 'gz')), may hold values from 0 to 15; in each aligned block of 16 rows (0 to 15, 16 to 31, ...) no two rows name the same one
- kdiag: float32 [32, 1024], P(('gx', 'gy', 'gz')), may hold values from 0.5 to 4
- rhs: float32 [32, 1024], P(('gx', 'gy', 'gz')), may hold values from -40 to 40
- modes: float32 [32, 6, 1024], P(('gx', 'gy', 'gz')), may hold values from -6 to 6
Outputs:
- schur: bfloat16 [32, 1024, 1024], P(('gx', 'gy', 'gz'))
- solution: float32 [32, 1024], P(('gx', 'gy', 'gz'))
- residual: float32 [32, 1024], P(('gx', 'gy', 'gz'))
Inputs may be any that keep to these rules, and one draw needn't show every extreme that they name: `owner`: the 16 blocks of one device go to different owners.
All inputs are finite; a program needn't handle non-finite values.
Results may differ from a plain program's by a relative error of at most 0.001.
Values may be sent and summed in bfloat16 or wider, within the bound.
A program may use at most 64 MiB of HBM per device.

v0:
```python
import jax
import jax.numpy as jnp
from jax import lax
from jax.sharding import PartitionSpec as P

ITERS = 2


def extended(block, sides, width):
    for axis, dim in sides:
        count = lax.axis_size(axis)
        forward = [(i, i + 1) for i in range(count - 1)]
        forward.append((count - 1, 0))
        backward = [(target, source) for source, target in forward]
        low = lax.ppermute(
            lax.slice_in_dim(block, block.shape[dim] - width, None, axis=dim), axis, forward
        )
        high = lax.ppermute(lax.slice_in_dim(block, 0, width, axis=dim), axis, backward)
        block = jnp.concatenate([low, block, high], axis=dim)
    return block


def add_faces(values, grid):
    width = values.shape[1]
    face = width // 8
    extra = jnp.concatenate(
        [
            grid[2, 1, 1][:, face : 2 * face],
            grid[0, 1, 1][:, 0:face],
            grid[1, 2, 1][:, 3 * face : 4 * face],
            grid[1, 0, 1][:, 2 * face : 3 * face],
            grid[1, 1, 2][:, 6 * face : 8 * face],
            grid[1, 1, 0][:, 4 * face : 6 * face],
        ],
        axis=1,
    )
    return values + extra


def shards(blocks, counts, owner, kdiag, rhs, modes):
    hi = lax.Precision.HIGHEST
    nblk, nrows, width = blocks.shape
    size_y = lax.axis_size("gy")
    size_z = lax.axis_size("gz")
    owners = size_y * size_z
    rowid = lax.broadcasted_iota(jnp.int32, (nblk, nrows, 1), 1)
    masked = jnp.where(rowid < counts[:, None, None], blocks, jnp.zeros_like(blocks))
    target = lax.broadcasted_iota(jnp.int32, (owners, nblk), 0)
    pick = (owner[:, 0][None, :] == target).astype(jnp.bfloat16)
    outgoing = jnp.dot(
        pick, masked.reshape(nblk, nrows * width), preferred_element_type=jnp.bfloat16
    )
    outgoing = outgoing.reshape(owners, nrows, width)
    arrived = lax.all_to_all(outgoing, ("gy", "gz"), split_axis=0, concat_axis=0, tiled=True)
    flat = arrived.reshape(owners * nrows, width)
    gram = lax.dot_general(flat, flat, (((0,), (0,)), ((), ())), preferred_element_type=jnp.float32)
    stiff = gram + jnp.diag(kdiag[0])
    schur = stiff.astype(jnp.bfloat16)[None]
    stacked = jnp.concatenate([rhs, modes[0]], axis=0)
    grid = extended(stacked[None, None, None], (("gx", 0), ("gy", 1), ("gz", 2)), 1)
    loaded = add_faces(stacked, grid)
    force = loaded[0]
    basis = loaded[1:]
    coarse, gforce, fnorm = lax.psum(
        (
            0.5 * jnp.dot(basis, basis.T, precision=hi),
            0.5 * jnp.dot(basis, force, precision=hi),
            0.5 * jnp.sum(force * force),
        ),
        ("gx", "gy", "gz"),
    )
    factor = jnp.linalg.cholesky(coarse)
    coef = jax.scipy.linalg.cho_solve((factor, True), gforce)
    residual = force - jnp.dot(coef, basis, precision=hi)
    norm_now = fnorm - jnp.dot(gforce, coef, precision=hi)
    direction = residual
    solution = jnp.zeros_like(force)
    for step in range(ITERS):
        local = jnp.dot(stiff, direction, precision=hi)
        faces = extended(local[None, None, None, None], (("gx", 0), ("gy", 1), ("gz", 2)), 1)
        image = add_faces(local[None], faces)[0]
        gimage, curve, square, cross = lax.psum(
            (
                0.5 * jnp.dot(basis, image, precision=hi),
                0.5 * jnp.sum(direction * image),
                0.5 * jnp.sum(image * image),
                0.5 * jnp.sum(residual * image),
            ),
            ("gx", "gy", "gz"),
        )
        coef = jax.scipy.linalg.cho_solve((factor, True), gimage)
        along = image - jnp.dot(coef, basis, precision=hi)
        alpha = norm_now / curve
        along_sq = (
            square
            - 2.0 * jnp.dot(coef, gimage, precision=hi)
            + jnp.dot(coef, jnp.dot(coarse, coef, precision=hi), precision=hi)
        )
        norm_next = norm_now - 2.0 * alpha * cross + alpha * alpha * along_sq
        solution = solution + alpha * direction
        residual = residual - alpha * along
        direction = residual + norm_next / norm_now * direction
        norm_now = norm_next
    return (schur, solution[None], residual[None])


def solution(mesh):
    in_specs = (
        P(("gx", "gy", "gz"), None, None),
        P(("gx", "gy", "gz")),
        P(("gx", "gy", "gz"), None),
        P(("gx", "gy", "gz"), None),
        P(("gx", "gy", "gz"), None),
        P(("gx", "gy", "gz"), None, None),
    )
    out_specs = (
        P(("gx", "gy", "gz"), None, None),
        P(("gx", "gy", "gz"), None),
        P(("gx", "gy", "gz"), None),
    )
    return jax.shard_map(shards, mesh=mesh, in_specs=in_specs, out_specs=out_specs, check_vma=False)
```

profile of v0, /device:TPU:12, one launch (start us, length us, event | category | flops | bytes accessed | tf_op | source)
XLA Modules:
  0.0 312.4 jit_solution(2874678932765971015)
XLA Ops:
  0.6 0.7 iota_compare_fusion.1
  1.4 2.5 broadcast_select_fusion
  3.9 3.0 fusion
  6.8 4.3 %copy.15 = bf16[16,128,1024]{2,1,0:T(8,128)(2,1)} copy(bf16[16,128,1024]{2,0,1:T(8,128)(2,1)S(1)} %fusion) | data formatting | bytes 8388608 | tf_op jit(solution)/shard_map/dot_general | solution.py:50
  11.1 6.4 %all-to-all-start = ((bf16[16,128,1024]{2,1,0:T(8,128)(2,1)}), bf16[16,128,1024]{2,1,0:T(8,128)(2,1)}, u32[]{:S(2)}, u32[]{:S(2)}) async-start(bf16[16,128,1024]{2,1,0:T(8,128)(2,1)} %copy.15), calls=%async_computation | async-start | bytes 8388608 | tf_op jit(solution)/shard_map/all_to_all | solution.py:54
  17.6 1.6 collective-permute-start
  19.1 0.5 collective-permute-start.1
  19.7 1.9 collective-permute-done
  21.5 1.5 collective-permute-done.1
  23.1 0.5 collective-permute-start.3
  23.6 16.4 %collective-permute-done.2 = f32[3,1,1,7,1024]{4,3,2,1,0:T(8,128)S(1)} collective-permute-done((f32[3,1,1,7,1024]{4,3,2,1,0:T(8,128)S(1)}, f32[3,1,1,7,1024]{4,3,2,1,0:T(8,128)S(1)}, u32[]{:S(2)}, u32[]{:S(2)}) %collective-permute-start.2) | collective-permute-done | bytes 86048 | tf_op jit(solution)/shard_map/ppermute | solution.py:18
  40.0 0.4 collective-permute-done.3
  40.5 19.8 %collective-permute-start.4 = (f32[3,3,1,7,1024]{4,3,2,1,0:T(8,128)S(1)}, f32[3,3,1,7,1024]{4,3,2,1,0:T(8,128)S(1)}, u32[]{:S(2)}, u32[]{:S(2)}) collective-permute-start(f32[3,3,1,7,1024]{4,3,2,1,0:T(8,128)S(1)} %pad_maximum_fusion), channel_id=1, source_target_pairs={{1,0},{2,1},{3,2},{0,3},{5,4},{6,5},{7,6},{4,7},{9,8},{10,9},{11,1... | collective-permute-start | bytes 774152 | tf_op jit(solution)/shard_map/ppermute | solution.py:18
  60.3 62.5 %collective-permute-done.4 = f32[3,3,1,7,1024]{4,3,2,1,0:T(8,128)S(1)} collective-permute-done((f32[3,3,1,7,1024]{4,3,2,1,0:T(8,128)S(1)}, f32[3,3,1,7,1024]{4,3,2,1,0:T(8,128)S(1)}, u32[]{:S(2)}, u32[]{:S(2)}) %collective-permute-start.4) | collective-permute-done | bytes 258080 | tf_op jit(solution)/shard_map/ppermute | solution.py:18
  122.8 0.2 fusion.13
  122.9 0.2 convolution_multiply_fusion
  123.1 39.6 %all-reduce.2 = (f32[6,6]{1,0:T(8,128)S(1)}, f32[6]{0:T(128)S(1)}) all-reduce(f32[6,6]{1,0:T(8,128)S(1)} %convolution_multiply_fusion, f32[6]{0:T(128)S(1)} %fusion.13), channel_id=1, replica_groups=mesh['gx'=2,'gy'=4,'gz'=4] {'gx','gy','gz'}, use_global_device_ids=true, to_apply=%region_3.4 | all-reduce | flops 42 | bytes 336 | tf_op jit(solution)/shard_map/psum | solution.py:64
  162.7 0.1 copy.10
  162.8 0.5 cholesky.18
  163.3 0.6 compare_reduce_fusion
  164.0 0.6 fusion.30
  164.7 0.5 custom-call.10
  165.1 0.1 convolution_bitcast_fusion.4
  165.2 0.8 fusion.48
  166.0 0.2 fusion.24
  166.2 0.6 multiply_reduce_fusion.3
  166.8 7.6 %fusion.53 = f32[1024,1024,1]{1,0,2:T(8,128)S(1)} fusion(bf16[16,128,1024]{2,1,0:T(8,128)(2,1)} %all-to-all-done), kind=kOutput, calls=%fused_computation.129 | convolution fusion | flops 4294967296 | bytes 8388608 | tf_op jit(solution)/shard_map/dot_general | solution.py:56
  174.4 1.9 copy-done
  176.3 3.7 %fusion.4 = f32[1,1024]{1,0:T(1,128)S(1)} fusion(f32[1024,1]{0,1:T(1,128)S(1)} %bitcast.222, f32[1024,1024,1]{1,0,2:T(8,128)S(1)} %fusion.53, f32[1024]{0:T(1024)S(1)} %bitcast.238), kind=kOutput, calls=%fused_computation.7 | convolution fusion | flops 15728640 | bytes 4206592 | tf_op jit(solution)/shard_map/dot_general | solution.py:79
  180.0 0.6 collective-permute-start.6
  180.6 1.5 collective-permute-start.7
  182.7 0.9 collective-permute-done.6
  183.6 0.6 collective-permute-done.7
  184.3 0.5 collective-permute-start.9
  184.8 0.9 collective-permute-done.8
  185.7 1.9 collective-permute-done.9
  187.6 2.1 collective-permute-start.10
  189.8 1.8 collective-permute-done.10
  191.6 2.1 collective-permute-done.11
  193.7 0.6 multiply_reduce_fusion.1
  195.0 0.2 fusion.12
  195.8 42.9 %all-reduce.1 = (f32[]{:T(128)}, f32[]{:T(128)}, f32[]{:T(128)}, f32[6]{0:T(128)S(1)}) all-reduce(f32[]{:T(128)S(6)} %mul.83, f32[]{:T(128)S(6)} %mul.88, f32[]{:T(128)S(6)} %mul.95, f32[6]{0:T(128)S(1)} %fusion.12), channel_id=1, replica_groups=mesh['gx'=2,'gy'=4,'gz'=4] {'gx','gy','gz'}, use_global_device_ids=true, to_apply=%region_1.2 | all-reduce | flops 9 | bytes 72 | tf_op jit(solution)/shard_map/psum | solution.py:64
  238.7 0.1 convolution_bitcast_fusion.3
  238.8 0.8 fusion.45
  239.6 0.8 fusion.15
  240.4 0.2 fusion.21
  245.2 5.9 %fusion.3 = f32[1,1024]{1,0:T(1,128)S(1)} fusion(f32[1024,1]{0,1:T(1,128)S(1)} %bitcast.223, f32[1024,1024,1]{1,0,2:T(8,128)} %copy-done, f32[1024]{0:T(1024)S(1)} %bitcast.239), kind=kOutput, calls=%fused_computation.6 | convolution fusion | flops 15728640 | bytes 4206592 | tf_op jit(solution)/shard_map/dot_general | solution.py:79
  251.0 0.7 collective-permute-start.12
  251.7 1.4 collective-permute-start.13
  253.1 1.6 collective-permute-done.12
  254.6 0.7 collective-permute-done.13
  255.4 0.5 collective-permute-start.15
  255.9 0.9 collective-permute-done.14
  256.8 1.8 collective-permute-done.15
  258.7 2.0 collective-permute-start.17
  260.7 2.3 collective-permute-done.16
  263.1 0.6 multiply_reduce_fusion
  264.3 0.2 fusion.11
  264.5 4.0 %fusion.6 = bf16[1,1024,1024]{2,1,0:T(8,128)(2,1)} fusion(f32[1024,1024,1]{1,0,2:T(8,128)} %copy-done, f32[1024]{0:T(1024)S(1)} %bitcast.240), kind=kLoop, calls=%fused_computation.9 | loop fusion | flops 4194304 | bytes 6295552 | tf_op jit(solution)/shard_map/broadcast_in_dim | solution.py:58
  268.4 42.2 %all-reduce = (f32[]{:T(128)}, f32[6]{0:T(128)S(1)}) all-reduce(f32[]{:T(128)S(6)} %mul.103, f32[6]{0:T(128)S(1)} %fusion.11), channel_id=1, replica_groups=mesh['gx'=2,'gy'=4,'gz'=4] {'gx','gy','gz'}, use_global_device_ids=true, to_apply=%region_12.14 | all-reduce | flops 7 | bytes 56 | tf_op jit(solution)/shard_map/psum | solution.py:82
  310.7 0.1 convolution_bitcast_fusion.1
  310.8 0.1 convolution_bitcast_fusion
  310.9 0.2 fusion.18
  311.8 0.6 multiply_subtract_fusion
  (67 shorter events, 0.6 us)
Async XLA Ops:
  1.4 2.5 copy-start.4
  11.1 6.4 %copy-start.2 = (f32[1,6,1024]{2,0,1:T(1,128)S(1)}, f32[1,6,1024]{2,0,1:T(1,128)}, u32[]{:S(2)}) copy-start(f32[1,6,1024]{2,0,1:T(1,128)} %param.13) | copy-start | bytes 73732
  11.1 6.4 %copy-start.3 = (f32[1,1024]{1,0:T(1,128)S(1)}, f32[1,1024]{1,0:T(1,128)}, u32[]{:S(2)}) copy-start(f32[1,1024]{1,0:T(1,128)} %param.12) | copy-start | bytes 12292
  11.1 155.6 %all-to-all-start = ((bf16[16,128,1024]{2,1,0:T(8,128)(2,1)}), bf16[16,128,1024]{2,1,0:T(8,128)(2,1)}, u32[]{:S(2)}, u32[]{:S(2)}) async-start(bf16[16,128,1024]{2,1,0:T(8,128)(2,1)} %copy.15), calls=%async_computation | async-start | bytes 8388608 | tf_op jit(solution)/shard_map/all_to_all | solution.py:54
  17.6 4.0 %collective-permute-start = (f32[1,1,1,7,1024]{4,3,2,1,0:T(8,128)S(1)}, f32[1,1,1,7,1024]{4,3,2,1,0:T(8,128)S(1)}, u32[]{:S(2)}, u32[]{:S(2)}) collective-permute-start(f32[1,1,1,7,1024]{4,3,2,1,0:T(8,128)S(1)} %fusion.17), channel_id=1, source_target_pairs={{16,0},{0,16},{17,1},{1,17},{18,2},{2,18},{19,3},{3,19},{20,4},{4,... | collective-permute-start | bytes 86024 | tf_op jit(solution)/shard_map/ppermute | solution.py:18
  19.1 3.9 %collective-permute-start.1 = (f32[1,1,1,7,1024]{4,3,2,1,0:T(8,128)S(1)}, f32[1,1,1,7,1024]{4,3,2,1,0:T(8,128)S(1)}, u32[]{:S(2)}, u32[]{:S(2)}) collective-permute-start(f32[1,1,1,7,1024]{4,3,2,1,0:T(8,128)S(1)} %fusion.17), channel_id=1, source_target_pairs={{0,16},{16,0},{1,17},{17,1},{2,18},{18,2},{3,19},{19,3},{4,20},{20... | collective-permute-start | bytes 86024 | tf_op jit(solution)/shard_map/ppermute | solution.py:15
  23.1 16.9 %collective-permute-start.2 = (f32[3,1,1,7,1024]{4,3,2,1,0:T(8,128)S(1)}, f32[3,1,1,7,1024]{4,3,2,1,0:T(8,128)S(1)}, u32[]{:S(2)}, u32[]{:S(2)}) collective-permute-start(f32[3,1,1,7,1024]{4,3,2,1,0:T(8,128)S(1)} %pad_maximum_fusion.1), channel_id=1, source_target_pairs={{4,0},{8,4},{12,8},{0,12},{5,1},{9,5},{13,9},{1,13},{6,2},{10,6},{... | collective-permute-start | bytes 258056 | tf_op jit(solution)/shard_map/ppermute | solution.py:18
  23.1 17.3 %collective-permute-start.3 = (f32[3,1,1,7,1024]{4,3,2,1,0:T(8,128)S(1)}, f32[3,1,1,7,1024]{4,3,2,1,0:T(8,128)S(1)}, u32[]{:S(2)}, u32[]{:S(2)}) collective-permute-start(f32[3,1,1,7,1024]{4,3,2,1,0:T(8,128)S(1)} %pad_maximum_fusion.1), channel_id=1, source_target_pairs={{0,4},{4,8},{8,12},{12,0},{1,5},{5,9},{9,13},{13,1},{2,6},{6,10},{... | collective-permute-start | bytes 258056 | tf_op jit(solution)/shard_map/ppermute | solution.py:15
  40.5 82.2 %collective-permute-start.4 = (f32[3,3,1,7,1024]{4,3,2,1,0:T(8,128)S(1)}, f32[3,3,1,7,1024]{4,3,2,1,0:T(8,128)S(1)}, u32[]{:S(2)}, u32[]{:S(2)}) collective-permute-start(f32[3,3,1,7,1024]{4,3,2,1,0:T(8,128)S(1)} %pad_maximum_fusion), channel_id=1, source_target_pairs={{1,0},{2,1},{3,2},{0,3},{5,4},{6,5},{7,6},{4,7},{9,8},{10,9},{11,1... | collective-permute-start | bytes 774152 | tf_op jit(solution)/shard_map/ppermute | solution.py:18
  60.2 62.5 %collective-permute-start.5 = (f32[3,3,1,7,1024]{4,3,2,1,0:T(8,128)S(1)}, f32[3,3,1,7,1024]{4,3,2,1,0:T(8,128)S(1)}, u32[]{:S(2)}, u32[]{:S(2)}) collective-permute-start(f32[3,3,1,7,1024]{4,3,2,1,0:T(8,128)S(1)} %pad_maximum_fusion), channel_id=1, source_target_pairs={{0,1},{1,2},{2,3},{3,0},{4,5},{5,6},{6,7},{7,4},{8,9},{9,10},{10,1... | collective-permute-start | bytes 774152 | tf_op jit(solution)/shard_map/ppermute | solution.py:15
  166.8 9.5 %copy-start.1 = (f32[1,1024]{1,0:T(1,128)S(1)}, f32[1,1024]{1,0:T(1,128)}, u32[]{:S(2)}) copy-start(f32[1,1024]{1,0:T(1,128)} %param.11) | copy-start | bytes 12292
  174.4 1.9 copy-start
  180.0 3.6 %collective-permute-start.6 = (f32[1,1,1,1,1024]{4,3,2,1,0:T(1,128)S(1)}, f32[1,1,1,1,1024]{4,3,2,1,0:T(1,128)S(1)}, u32[]{:S(2)}, u32[]{:S(2)}) collective-permute-start(f32[1,1,1,1,1024]{4,3,2,1,0:T(1,128)S(1)} %bitcast.224), channel_id=1, source_target_pairs={{16,0},{0,16},{17,1},{1,17},{18,2},{2,18},{19,3},{3,19},{20,4},{4,... | collective-permute-start | bytes 12296 | tf_op jit(solution)/shard_map/ppermute | solution.py:18
  180.6 3.6 %collective-permute-start.7 = (f32[1,1,1,1,1024]{4,3,2,1,0:T(1,128)S(1)}, f32[1,1,1,1,1024]{4,3,2,1,0:T(1,128)S(1)}, u32[]{:S(2)}, u32[]{:S(2)}) collective-permute-start(f32[1,1,1,1,1024]{4,3,2,1,0:T(1,128)S(1)} %bitcast.225), channel_id=1, source_target_pairs={{0,16},{16,0},{1,17},{17,1},{2,18},{18,2},{3,19},{19,3},{4,20},{20... | collective-permute-start | bytes 12296 | tf_op jit(solution)/shard_map/ppermute | solution.py:15
  184.2 1.5 collective-permute-start.8
  184.3 3.3 %collective-permute-start.9 = (f32[3,1,1,1,1024]{4,3,2,1,0:T(1,128)S(1)}, f32[3,1,1,1,1024]{4,3,2,1,0:T(1,128)S(1)}, u32[]{:S(2)}, u32[]{:S(2)}) collective-permute-start(f32[3,1,1,1,1024]{4,3,2,1,0:T(1,128)S(1)} %pad_maximum_fusion.5), channel_id=1, source_target_pairs={{0,4},{4,8},{8,12},{12,0},{1,5},{5,9},{9,13},{13,1},{2,6},{6,10},{... | collective-permute-start | bytes 36872 | tf_op jit(solution)/shard_map/ppermute | solution.py:15
  187.6 4.0 %collective-permute-start.10 = (f32[3,3,1,1,1024]{4,3,2,1,0:T(1,128)S(1)}, f32[3,3,1,1,1024]{4,3,2,1,0:T(1,128)S(1)}, u32[]{:S(2)}, u32[]{:S(2)}) collective-permute-start(f32[3,3,1,1,1024]{4,3,2,1,0:T(1,128)S(1)} %pad_maximum_fusion.2), channel_id=1, source_target_pairs={{1,0},{2,1},{3,2},{0,3},{5,4},{6,5},{7,6},{4,7},{9,8},{10,9},{11,1... | collective-permute-start | bytes 110600 | tf_op jit(solution)/shard_map/ppermute | solution.py:18
  189.7 4.0 %collective-permute-start.11 = (f32[3,3,1,1,1024]{4,3,2,1,0:T(1,128)S(1)}, f32[3,3,1,1,1024]{4,3,2,1,0:T(1,128)S(1)}, u32[]{:S(2)}, u32[]{:S(2)}) collective-permute-start(f32[3,3,1,1,1024]{4,3,2,1,0:T(1,128)S(1)} %pad_maximum_fusion.2), channel_id=1, source_target_pairs={{0,1},{1,2},{2,3},{3,0},{4,5},{5,6},{6,7},{7,4},{8,9},{9,10},{10,1... | collective-permute-start | bytes 110600 | tf_op jit(solution)/shard_map/ppermute | solution.py:15
  251.0 3.6 %collective-permute-start.12 = (f32[1,1,1,1,1024]{4,3,2,1,0:T(1,128)S(1)}, f32[1,1,1,1,1024]{4,3,2,1,0:T(1,128)S(1)}, u32[]{:S(2)}, u32[]{:S(2)}) collective-permute-start(f32[1,1,1,1,1024]{4,3,2,1,0:T(1,128)S(1)} %bitcast.229), channel_id=1, source_target_pairs={{16,0},{0,16},{17,1},{1,17},{18,2},{2,18},{19,3},{3,19},{20,4},{4,... | collective-permute-start | bytes 12296 | tf_op jit(solution)/shard_map/ppermute | solution.py:18
  251.7 3.6 %collective-permute-start.13 = (f32[1,1,1,1,1024]{4,3,2,1,0:T(1,128)S(1)}, f32[1,1,1,1,1024]{4,3,2,1,0:T(1,128)S(1)}, u32[]{:S(2)}, u32[]{:S(2)}) collective-permute-start(f32[1,1,1,1,1024]{4,3,2,1,0:T(1,128)S(1)} %bitcast.230), channel_id=1, source_target_pairs={{0,16},{16,0},{1,17},{17,1},{2,18},{18,2},{3,19},{19,3},{4,20},{20... | collective-permute-start | bytes 12296 | tf_op jit(solution)/shard_map/ppermute | solution.py:15
  255.3 1.5 collective-permute-start.14
  255.4 3.2 %collective-permute-start.15 = (f32[3,1,1,1,1024]{4,3,2,1,0:T(1,128)S(1)}, f32[3,1,1,1,1024]{4,3,2,1,0:T(1,128)S(1)}, u32[]{:S(2)}, u32[]{:S(2)}) collective-permute-start(f32[3,1,1,1,1024]{4,3,2,1,0:T(1,128)S(1)} %pad_maximum_fusion.6), channel_id=1, source_target_pairs={{0,4},{4,8},{8,12},{12,0},{1,5},{5,9},{9,13},{13,1},{2,6},{6,10},{... | collective-permute-start | bytes 36872 | tf_op jit(solution)/shard_map/ppermute | solution.py:15
  258.6 4.4 %collective-permute-start.16 = (f32[3,3,1,1,1024]{4,3,2,1,0:T(1,128)S(1)}, f32[3,3,1,1,1024]{4,3,2,1,0:T(1,128)S(1)}, u32[]{:S(2)}, u32[]{:S(2)}) collective-permute-start(f32[3,3,1,1,1024]{4,3,2,1,0:T(1,128)S(1)} %pad_maximum_fusion.3), channel_id=1, source_target_pairs={{1,0},{2,1},{3,2},{0,3},{5,4},{6,5},{7,6},{4,7},{9,8},{10,9},{11,1... | collective-permute-start | bytes 110600 | tf_op jit(solution)/shard_map/ppermute | solution.py:18
  258.7 4.4 %collective-permute-start.17 = (f32[3,3,1,1,1024]{4,3,2,1,0:T(1,128)S(1)}, f32[3,3,1,1,1024]{4,3,2,1,0:T(1,128)S(1)}, u32[]{:S(2)}, u32[]{:S(2)}) collective-permute-start(f32[3,3,1,1,1024]{4,3,2,1,0:T(1,128)S(1)} %pad_maximum_fusion.3), channel_id=1, source_target_pairs={{0,1},{1,2},{2,3},{3,0},{4,5},{5,6},{6,7},{7,4},{8,9},{9,10},{10,1... | collective-permute-start | bytes 110600 | tf_op jit(solution)/shard_map/ppermute | solution.py:15
where the time goes:
time: 313 us; the launch traced here: 312 us
  blocking collectives  125 us (40%)
  waiting for transfers between devices  98 us (31%)
  starting transfers between devices  38.2 us (12%)
  matrix products  24.1 us (8%)
  other arithmetic  12.1 us (4%)
  between operations  8.84 us (3%)
  local copies, waits for them, and re-layouts  6.48 us (2%)
    ppermute x9, waiting for transfers between devices, extended(): lax.ppermute(lax.slice_in_dim(block, 0, width, axis=dim), axis, backward)  89.1 us
    psum x2, blocking collectives, shards(): lax.psum((0.5 * jnp.dot(basis, basis.T, precision=hi), 0.5 * jnp.dot(basi...  82.4 us
    psum x1, blocking collectives, shards(): lax.psum((0.5 * jnp.dot(basis, image, precision=hi), 0.5 * jnp.sum(direct...  42.2 us
    ppermute x9, starting transfers between devices, extended(): lax.ppermute(lax.slice_in_dim(block, 0, width, axis=dim), axis, backward)  25 us
    dot_general x2, matrix products, shards(): local = jnp.dot(stiff, direction, precision=hi)  9.54 us
    ppermute x9, waiting for transfers between devices, extended(): lax.ppermute(lax.slice_in_dim(block, block.shape[dim] - width, None, axis...  8.88 us
    dot_general x1, matrix products, shards(): lax.dot_general(flat, flat, (((0,), (0,)), ((), ())), preferred_element_t...  7.58 us
    ppermute x9, starting transfers between devices, extended(): lax.ppermute(lax.slice_in_dim(block, block.shape[dim] - width, None, axis...  6.87 us
  transfers between devices with their start and end apart: 19, of which 16 were waited for; matrix products, arithmetic and copies ran while one was open for 1% of the time, Pallas kernels for 0%

commit v1 on v0

--- a/solution.py
+++ b/solution.py
@@ -80,13 +80,16 @@
         faces = extended(local[None, None, None, None], (("gx", 0), ("gy", 1), ("gz", 2)), 1)
         image = add_faces(local[None], faces)[0]
         gimage, curve, square, cross = lax.psum(
-            (
-                0.5 * jnp.dot(basis, image, precision=hi),
-                0.5 * jnp.sum(direction * image),
-                0.5 * jnp.sum(image * image),
-                0.5 * jnp.sum(residual * image),
+            lax.psum(
+                (
+                    0.5 * jnp.dot(basis, image, precision=hi),
+                    0.5 * jnp.sum(direction * image),
+                    0.5 * jnp.sum(image * image),
+                    0.5 * jnp.sum(residual * image),
+                ),
+                ("gy", "gz"),
             ),
-            ("gx", "gy", "gz"),
+            "gx",
         )
         coef = jax.scipy.linalg.cho_solve((factor, True), gimage)
         along = image - jnp.dot(coef, basis, precision=hi)

time: 313 us -> 308 us (0.984)
  blocking collectives: 125 us -> 118 us
    psum x2 -> x1, blocking collectives: 82.4 us -> 39.9 us  [shards(): lax.psum((0.5 * jnp.dot(basis, basis.T, precision=hi), 0.5 * jnp.dot(basi...]
    psum x1 -> x2, blocking collectives: 42.2 us -> 67 us  [shards(): lax.psum((0.5 * jnp.dot(basis, image, precision=hi), 0.5 * jnp.sum(direct...]
    psum x0 -> x2, blocking collectives: none -> 11.1 us  [shards(): lax.psum(lax.psum((0.5 * jnp.dot(basis, image, precision=hi), 0.5 * jnp.s...]
  transfers between devices with their start and end apart: 19 -> 19, of which waited for: 16 -> 17; matrix products, arithmetic and copies ran while one was open for 1% -> 1% of each run, Pallas kernels for 0% -> 0%
where the time goes in v1:
time: 308 us; the launch traced here: 307 us
  blocking collectives  118 us (38%)
  waiting for transfers between devices  99 us (32%)
  starting transfers between devices  38.2 us (12%)
  matrix products  24 us (8%)
  other arithmetic  12.1 us (4%)
  between operations  8.86 us (3%)
  local copies, waits for them, and re-layouts  6.48 us (2%)
    ppermute x9, waiting for transfers between devices, extended(): lax.ppermute(lax.slice_in_dim(block, 0, width, axis=dim), axis, backward)  89.4 us
    psum x2, blocking collectives, shards(): lax.psum((0.5 * jnp.dot(basis, image, precision=hi), 0.5 * jnp.sum(direct...  67 us
    psum x1, blocking collectives, shards(): lax.psum((0.5 * jnp.dot(basis, basis.T, precision=hi), 0.5 * jnp.dot(basi...  39.9 us
    ppermute x9, starting transfers between devices, extended(): lax.ppermute(lax.slice_in_dim(block, 0, width, axis=dim), axis, backward)  25.8 us
    psum x2, blocking collectives, shards(): lax.psum(lax.psum((0.5 * jnp.dot(basis, image, precision=hi), 0.5 * jnp.s...  11.1 us
    ppermute x9, waiting for transfers between devices, extended(): lax.ppermute(lax.slice_in_dim(block, block.shape[dim] - width, None, axis...  9.64 us
    dot_general x2, matrix products, shards(): local = jnp.dot(stiff, direction, precision=hi)  9.54 us
    dot_general x1, matrix products, shards(): lax.dot_general(flat, flat, (((0,), (0,)), ((), ())), preferred_element_t...  7.6 us
  transfers between devices with their start and end apart: 19, of which 17 were waited for; matrix products, arithmetic and copies ran while one was open for 1% of the time, Pallas kernels for 0%

profile of v1, /device:TPU:12, one launch (start us, length us, event | category | flops | bytes accessed | tf_op | source)
XLA Modules:
  0.0 306.6 jit_solution(18298964921047866385)
XLA Ops:
  0.6 0.7 iota_compare_fusion.1
  1.4 2.5 broadcast_select_fusion
  3.9 3.0 fusion
  6.8 4.3 %copy.15 = bf16[16,128,1024]{2,1,0:T(8,128)(2,1)} copy(bf16[16,128,1024]{2,0,1:T(8,128)(2,1)S(1)} %fusion) | data formatting | bytes 8388608 | tf_op jit(solution)/shard_map/dot_general | solution.py:50
  11.1 6.4 %all-to-all-start = ((bf16[16,128,1024]{2,1,0:T(8,128)(2,1)}), bf16[16,128,1024]{2,1,0:T(8,128)(2,1)}, u32[]{:S(2)}, u32[]{:S(2)}) async-start(bf16[16,128,1024]{2,1,0:T(8,128)(2,1)} %copy.15), calls=%async_computation | async-start | bytes 8388608 | tf_op jit(solution)/shard_map/all_to_all | solution.py:54
  17.6 1.6 collective-permute-start
  19.1 0.5 collective-permute-start.1
  19.7 1.9 collective-permute-done
  21.5 1.5 collective-permute-done.1
  23.1 0.5 collective-permute-start.3
  23.6 16.4 %collective-permute-done.2 = f32[3,1,1,7,1024]{4,3,2,1,0:T(8,128)S(1)} collective-permute-done((f32[3,1,1,7,1024]{4,3,2,1,0:T(8,128)S(1)}, f32[3,1,1,7,1024]{4,3,2,1,0:T(8,128)S(1)}, u32[]{:S(2)}, u32[]{:S(2)}) %collective-permute-start.2) | collective-permute-done | bytes 86048 | tf_op jit(solution)/shard_map/ppermute | solution.py:18
  40.0 0.4 collective-permute-done.3
  40.5 19.8 %collective-permute-start.4 = (f32[3,3,1,7,1024]{4,3,2,1,0:T(8,128)S(1)}, f32[3,3,1,7,1024]{4,3,2,1,0:T(8,128)S(1)}, u32[]{:S(2)}, u32[]{:S(2)}) collective-permute-start(f32[3,3,1,7,1024]{4,3,2,1,0:T(8,128)S(1)} %pad_maximum_fusion), channel_id=1, source_target_pairs={{1,0},{2,1},{3,2},{0,3},{5,4},{6,5},{7,6},{4,7},{9,8},{10,9},{11,1... | collective-permute-start | bytes 774152 | tf_op jit(solution)/shard_map/ppermute | solution.py:18
  60.3 62.5 %collective-permute-done.4 = f32[3,3,1,7,1024]{4,3,2,1,0:T(8,128)S(1)} collective-permute-done((f32[3,3,1,7,1024]{4,3,2,1,0:T(8,128)S(1)}, f32[3,3,1,7,1024]{4,3,2,1,0:T(8,128)S(1)}, u32[]{:S(2)}, u32[]{:S(2)}) %collective-permute-start.4) | collective-permute-done | bytes 258080 | tf_op jit(solution)/shard_map/ppermute | solution.py:18
  122.8 0.6 multiply_reduce_fusion.3
  123.4 0.1 convolution_multiply_fusion
  123.5 0.2 fusion.13
  124.4 39.9 %all-reduce = (f32[6,6]{1,0:T(8,128)S(1)}, f32[6]{0:T(128)S(1)}, f32[]{:T(128)}) all-reduce(f32[6,6]{1,0:T(8,128)S(1)} %convolution_multiply_fusion, f32[6]{0:T(128)S(1)} %fusion.13, f32[]{:T(128)S(6)} %mul.83), channel_id=1, replica_groups=mesh['gx'=2,'gy'=4,'gz'=4] {'gx','gy','gz'}, use_global_device_ids=true, to_apply=%region_3.4 | all-reduce | flops 43 | bytes 344 | tf_op jit(solution)/shard_map/psum | solution.py:64
  164.4 0.5 cholesky.18
  164.9 0.6 compare_reduce_fusion
  165.6 0.6 fusion.30
  166.2 0.5 custom-call.10
  166.7 0.1 convolution_bitcast_fusion.4
  166.8 0.8 fusion.48
  167.6 0.2 fusion.24
  167.8 7.6 %fusion.53 = f32[1024,1024,1]{1,0,2:T(8,128)S(1)} fusion(bf16[16,128,1024]{2,1,0:T(8,128)(2,1)} %all-to-all-done), kind=kOutput, calls=%fused_computation.129 | convolution fusion | flops 4294967296 | bytes 8388608 | tf_op jit(solution)/shard_map/dot_general | solution.py:56
  175.4 1.9 copy-done
  177.3 3.7 %fusion.4 = f32[1,1024]{1,0:T(1,128)S(1)} fusion(f32[1024,1]{0,1:T(1,128)S(1)} %bitcast.222, f32[1024,1024,1]{1,0,2:T(8,128)S(1)} %fusion.53, f32[1024]{0:T(1024)S(1)} %bitcast.240), kind=kOutput, calls=%fused_computation.7 | convolution fusion | flops 15728640 | bytes 4206592 | tf_op jit(solution)/shard_map/dot_general | solution.py:79
  181.0 0.6 collective-permute-start.6
  181.6 1.5 collective-permute-start.7
  183.1 1.6 collective-permute-done.6
  184.6 0.6 collective-permute-done.7
  185.3 0.5 collective-permute-start.9
  185.8 0.9 collective-permute-done.8
  186.7 1.8 collective-permute-done.9
  188.5 2.1 collective-permute-start.10
  190.7 1.8 collective-permute-done.10
  192.5 2.1 collective-permute-done.11
  194.6 0.6 multiply_reduce_fusion.1
  196.5 0.2 fusion.12
  198.0 33.8 %all-reduce.2 = (f32[]{:T(128)}, f32[]{:T(128)}, f32[6]{0:T(128)S(1)}) all-reduce(f32[]{:T(128)S(6)} %mul.88, f32[]{:T(128)S(6)} %mul.95, f32[6]{0:T(128)S(1)} %fusion.12), channel_id=1, replica_groups=mesh['gx'=2,'gy'=4,'gz'=4] {'gy','gz'}, use_global_device_ids=true, to_apply=%region_7.9 | all-reduce | flops 8 | bytes 64 | tf_op jit(solution)/shard_map/psum | solution.py:83
  231.8 5.5 %all-reduce.4 = (f32[]{:T(128)}, f32[]{:T(128)}, f32[6]{0:T(128)S(1)}) all-reduce(f32[]{:T(128)} %get-tuple-element.11, f32[]{:T(128)} %get-tuple-element.12, f32[6]{0:T(128)S(1)} %get-tuple-element.13), channel_id=1, replica_groups=mesh['gx'=2,'gy'=4,'gz'=4] {'gx'}, use_global_device_ids=true, to_apply=%region_8.10 | all-reduce | flops 8 | bytes 64 | tf_op jit(solution)/shard_map/psum | solution.py:82
  237.5 0.7 fusion.45
  238.2 0.7 fusion.15
  238.9 0.2 fusion.21
  242.4 5.9 %fusion.3 = f32[1,1024]{1,0:T(1,128)S(1)} fusion(f32[1024,1]{0,1:T(1,128)S(1)} %bitcast.223, f32[1024,1024,1]{1,0,2:T(8,128)} %copy-done, f32[1024]{0:T(1024)S(1)} %bitcast.241), kind=kOutput, calls=%fused_computation.6 | convolution fusion | flops 15728640 | bytes 4206592 | tf_op jit(solution)/shard_map/dot_general | solution.py:79
  248.3 1.5 collective-permute-start.12
  249.8 0.6 collective-permute-start.13
  250.3 1.6 collective-permute-done.12
  251.9 1.5 collective-permute-done.13
  253.4 0.5 collective-permute-start.15
  254.0 0.9 collective-permute-done.14
  254.8 1.8 collective-permute-done.15
  256.7 2.0 collective-permute-start.17
  258.8 1.9 collective-permute-done.16
  260.8 0.6 multiply_reduce_fusion
  262.0 0.2 fusion.11
  262.2 4.0 %fusion.6 = bf16[1,1024,1024]{2,1,0:T(8,128)(2,1)} fusion(f32[1024,1024,1]{1,0,2:T(8,128)} %copy-done, f32[1024]{0:T(1024)S(1)} %bitcast.242), kind=kLoop, calls=%fused_computation.9 | loop fusion | flops 4194304 | bytes 6295552 | tf_op jit(solution)/shard_map/broadcast_in_dim | solution.py:58
  266.1 33.2 %all-reduce.1 = (f32[]{:T(128)}, f32[6]{0:T(128)S(1)}) all-reduce(f32[]{:T(128)S(6)} %mul.103, f32[6]{0:T(128)S(1)} %fusion.11), channel_id=1, replica_groups=mesh['gx'=2,'gy'=4,'gz'=4] {'gy','gz'}, use_global_device_ids=true, to_apply=%region_15.17 | all-reduce | flops 7 | bytes 56 | tf_op jit(solution)/shard_map/psum | solution.py:83
  299.3 5.5 %all-reduce.3 = (f32[]{:T(128)}, f32[6]{0:T(128)S(1)}) all-reduce(f32[]{:T(128)} %get-tuple-element.9, f32[6]{0:T(128)S(1)} %get-tuple-element.10), channel_id=1, replica_groups=mesh['gx'=2,'gy'=4,'gz'=4] {'gx'}, use_global_device_ids=true, to_apply=%region_16.18 | all-reduce | flops 7 | bytes 56 | tf_op jit(solution)/shard_map/psum | solution.py:82
  304.8 0.1 convolution_bitcast_fusion.1
  305.0 0.1 convolution_bitcast_fusion
  305.1 0.2 fusion.18
  306.0 0.6 multiply_subtract_fusion
  (70 shorter events, 0.9 us)
Async XLA Ops:
  1.4 2.5 copy-start.4
  11.1 6.4 %copy-start.2 = (f32[1,6,1024]{2,0,1:T(1,128)S(1)}, f32[1,6,1024]{2,0,1:T(1,128)}, u32[]{:S(2)}) copy-start(f32[1,6,1024]{2,0,1:T(1,128)} %param.13) | copy-start | bytes 73732
  11.1 6.4 %copy-start.3 = (f32[1,1024]{1,0:T(1,128)S(1)}, f32[1,1024]{1,0:T(1,128)}, u32[]{:S(2)}) copy-start(f32[1,1024]{1,0:T(1,128)} %param.12) | copy-start | bytes 12292
  11.1 156.6 %all-to-all-start = ((bf16[16,128,1024]{2,1,0:T(8,128)(2,1)}), bf16[16,128,1024]{2,1,0:T(8,128)(2,1)}, u32[]{:S(2)}, u32[]{:S(2)}) async-start(bf16[16,128,1024]{2,1,0:T(8,128)(2,1)} %copy.15), calls=%async_computation | async-start | bytes 8388608 | tf_op jit(solution)/shard_map/all_to_all | solution.py:54
  17.6 4.0 %collective-permute-start = (f32[1,1,1,7,1024]{4,3,2,1,0:T(8,128)S(1)}, f32[1,1,1,7,1024]{4,3,2,1,0:T(8,128)S(1)}, u32[]{:S(2)}, u32[]{:S(2)}) collective-permute-start(f32[1,1,1,7,1024]{4,3,2,1,0:T(8,128)S(1)} %fusion.17), channel_id=1, source_target_pairs={{16,0},{0,16},{17,1},{1,17},{18,2},{2,18},{19,3},{3,19},{20,4},{4,... | collective-permute-start | bytes 86024 | tf_op jit(solution)/shard_map/ppermute | solution.py:18
  19.1 3.9 %collective-permute-start.1 = (f32[1,1,1,7,1024]{4,3,2,1,0:T(8,128)S(1)}, f32[1,1,1,7,1024]{4,3,2,1,0:T(8,128)S(1)}, u32[]{:S(2)}, u32[]{:S(2)}) collective-permute-start(f32[1,1,1,7,1024]{4,3,2,1,0:T(8,128)S(1)} %fusion.17), channel_id=1, source_target_pairs={{0,16},{16,0},{1,17},{17,1},{2,18},{18,2},{3,19},{19,3},{4,20},{20... | collective-permute-start | bytes 86024 | tf_op jit(solution)/shard_map/ppermute | solution.py:15
  23.1 16.9 %collective-permute-start.2 = (f32[3,1,1,7,1024]{4,3,2,1,0:T(8,128)S(1)}, f32[3,1,1,7,1024]{4,3,2,1,0:T(8,128)S(1)}, u32[]{:S(2)}, u32[]{:S(2)}) collective-permute-start(f32[3,1,1,7,1024]{4,3,2,1,0:T(8,128)S(1)} %pad_maximum_fusion.1), channel_id=1, source_target_pairs={{4,0},{8,4},{12,8},{0,12},{5,1},{9,5},{13,9},{1,13},{6,2},{10,6},{... | collective-permute-start | bytes 258056 | tf_op jit(solution)/shard_map/ppermute | solution.py:18
  23.1 17.3 %collective-permute-start.3 = (f32[3,1,1,7,1024]{4,3,2,1,0:T(8,128)S(1)}, f32[3,1,1,7,1024]{4,3,2,1,0:T(8,128)S(1)}, u32[]{:S(2)}, u32[]{:S(2)}) collective-permute-start(f32[3,1,1,7,1024]{4,3,2,1,0:T(8,128)S(1)} %pad_maximum_fusion.1), channel_id=1, source_target_pairs={{0,4},{4,8},{8,12},{12,0},{1,5},{5,9},{9,13},{13,1},{2,6},{6,10},{... | collective-permute-start | bytes 258056 | tf_op jit(solution)/shard_map/ppermute | solution.py:15
  40.5 82.2 %collective-permute-start.4 = (f32[3,3,1,7,1024]{4,3,2,1,0:T(8,128)S(1)}, f32[3,3,1,7,1024]{4,3,2,1,0:T(8,128)S(1)}, u32[]{:S(2)}, u32[]{:S(2)}) collective-permute-start(f32[3,3,1,7,1024]{4,3,2,1,0:T(8,128)S(1)} %pad_maximum_fusion), channel_id=1, source_target_pairs={{1,0},{2,1},{3,2},{0,3},{5,4},{6,5},{7,6},{4,7},{9,8},{10,9},{11,1... | collective-permute-start | bytes 774152 | tf_op jit(solution)/shard_map/ppermute | solution.py:18
  60.2 62.5 %collective-permute-start.5 = (f32[3,3,1,7,1024]{4,3,2,1,0:T(8,128)S(1)}, f32[3,3,1,7,1024]{4,3,2,1,0:T(8,128)S(1)}, u32[]{:S(2)}, u32[]{:S(2)}) collective-permute-start(f32[3,3,1,7,1024]{4,3,2,1,0:T(8,128)S(1)} %pad_maximum_fusion), channel_id=1, source_target_pairs={{0,1},{1,2},{2,3},{3,0},{4,5},{5,6},{6,7},{7,4},{8,9},{9,10},{10,1... | collective-permute-start | bytes 774152 | tf_op jit(solution)/shard_map/ppermute | solution.py:15
  167.7 9.6 %copy-start.1 = (f32[1,1024]{1,0:T(1,128)S(1)}, f32[1,1024]{1,0:T(1,128)}, u32[]{:S(2)}) copy-start(f32[1,1024]{1,0:T(1,128)} %param.11) | copy-start | bytes 12292
  175.4 1.9 copy-start
  181.0 3.6 %collective-permute-start.6 = (f32[1,1,1,1,1024]{4,3,2,1,0:T(1,128)S(1)}, f32[1,1,1,1,1024]{4,3,2,1,0:T(1,128)S(1)}, u32[]{:S(2)}, u32[]{:S(2)}) collective-permute-start(f32[1,1,1,1,1024]{4,3,2,1,0:T(1,128)S(1)} %bitcast.224), channel_id=1, source_target_pairs={{16,0},{0,16},{17,1},{1,17},{18,2},{2,18},{19,3},{3,19},{20,4},{4,... | collective-permute-start | bytes 12296 | tf_op jit(solution)/shard_map/ppermute | solution.py:18
  181.6 3.6 %collective-permute-start.7 = (f32[1,1,1,1,1024]{4,3,2,1,0:T(1,128)S(1)}, f32[1,1,1,1,1024]{4,3,2,1,0:T(1,128)S(1)}, u32[]{:S(2)}, u32[]{:S(2)}) collective-permute-start(f32[1,1,1,1,1024]{4,3,2,1,0:T(1,128)S(1)} %bitcast.225), channel_id=1, source_target_pairs={{0,16},{16,0},{1,17},{17,1},{2,18},{18,2},{3,19},{19,3},{4,20},{20... | collective-permute-start | bytes 12296 | tf_op jit(solution)/shard_map/ppermute | solution.py:15
  185.2 1.5 collective-permute-start.8
  185.3 3.2 %collective-permute-start.9 = (f32[3,1,1,1,1024]{4,3,2,1,0:T(1,128)S(1)}, f32[3,1,1,1,1024]{4,3,2,1,0:T(1,128)S(1)}, u32[]{:S(2)}, u32[]{:S(2)}) collective-permute-start(f32[3,1,1,1,1024]{4,3,2,1,0:T(1,128)S(1)} %pad_maximum_fusion.5), channel_id=1, source_target_pairs={{0,4},{4,8},{8,12},{12,0},{1,5},{5,9},{9,13},{13,1},{2,6},{6,10},{... | collective-permute-start | bytes 36872 | tf_op jit(solution)/shard_map/ppermute | solution.py:15
  188.5 4.0 %collective-permute-start.10 = (f32[3,3,1,1,1024]{4,3,2,1,0:T(1,128)S(1)}, f32[3,3,1,1,1024]{4,3,2,1,0:T(1,128)S(1)}, u32[]{:S(2)}, u32[]{:S(2)}) collective-permute-start(f32[3,3,1,1,1024]{4,3,2,1,0:T(1,128)S(1)} %pad_maximum_fusion.2), channel_id=1, source_target_pairs={{1,0},{2,1},{3,2},{0,3},{5,4},{6,5},{7,6},{4,7},{9,8},{10,9},{11,1... | collective-permute-start | bytes 110600 | tf_op jit(solution)/shard_map/ppermute | solution.py:18
  190.6 4.0 %collective-permute-start.11 = (f32[3,3,1,1,1024]{4,3,2,1,0:T(1,128)S(1)}, f32[3,3,1,1,1024]{4,3,2,1,0:T(1,128)S(1)}, u32[]{:S(2)}, u32[]{:S(2)}) collective-permute-start(f32[3,3,1,1,1024]{4,3,2,1,0:T(1,128)S(1)} %pad_maximum_fusion.2), channel_id=1, source_target_pairs={{0,1},{1,2},{2,3},{3,0},{4,5},{5,6},{6,7},{7,4},{8,9},{9,10},{10,1... | collective-permute-start | bytes 110600 | tf_op jit(solution)/shard_map/ppermute | solution.py:15
  248.3 3.6 %collective-permute-start.12 = (f32[1,1,1,1,1024]{4,3,2,1,0:T(1,128)S(1)}, f32[1,1,1,1,1024]{4,3,2,1,0:T(1,128)S(1)}, u32[]{:S(2)}, u32[]{:S(2)}) collective-permute-start(f32[1,1,1,1,1024]{4,3,2,1,0:T(1,128)S(1)} %bitcast.229), channel_id=1, source_target_pairs={{16,0},{0,16},{17,1},{1,17},{18,2},{2,18},{19,3},{3,19},{20,4},{4,... | collective-permute-start | bytes 12296 | tf_op jit(solution)/shard_map/ppermute | solution.py:18
  249.8 3.6 %collective-permute-start.13 = (f32[1,1,1,1,1024]{4,3,2,1,0:T(1,128)S(1)}, f32[1,1,1,1,1024]{4,3,2,1,0:T(1,128)S(1)}, u32[]{:S(2)}, u32[]{:S(2)}) collective-permute-start(f32[1,1,1,1,1024]{4,3,2,1,0:T(1,128)S(1)} %bitcast.230), channel_id=1, source_target_pairs={{0,16},{16,0},{1,17},{17,1},{2,18},{18,2},{3,19},{19,3},{4,20},{20... | collective-permute-start | bytes 12296 | tf_op jit(solution)/shard_map/ppermute | solution.py:15
  253.4 1.5 collective-permute-start.14
  253.4 3.2 %collective-permute-start.15 = (f32[3,1,1,1,1024]{4,3,2,1,0:T(1,128)S(1)}, f32[3,1,1,1,1024]{4,3,2,1,0:T(1,128)S(1)}, u32[]{:S(2)}, u32[]{:S(2)}) collective-permute-start(f32[3,1,1,1,1024]{4,3,2,1,0:T(1,128)S(1)} %pad_maximum_fusion.6), channel_id=1, source_target_pairs={{0,4},{4,8},{8,12},{12,0},{1,5},{5,9},{9,13},{13,1},{2,6},{6,10},{... | collective-permute-start | bytes 36872 | tf_op jit(solution)/shard_map/ppermute | solution.py:15
  256.7 4.0 %collective-permute-start.16 = (f32[3,3,1,1,1024]{4,3,2,1,0:T(1,128)S(1)}, f32[3,3,1,1,1024]{4,3,2,1,0:T(1,128)S(1)}, u32[]{:S(2)}, u32[]{:S(2)}) collective-permute-start(f32[3,3,1,1,1024]{4,3,2,1,0:T(1,128)S(1)} %pad_maximum_fusion.3), channel_id=1, source_target_pairs={{1,0},{2,1},{3,2},{0,3},{5,4},{6,5},{7,6},{4,7},{9,8},{10,9},{11,1... | collective-permute-start | bytes 110600 | tf_op jit(solution)/shard_map/ppermute | solution.py:18
  256.7 4.0 %collective-permute-start.17 = (f32[3,3,1,1,1024]{4,3,2,1,0:T(1,128)S(1)}, f32[3,3,1,1,1024]{4,3,2,1,0:T(1,128)S(1)}, u32[]{:S(2)}, u32[]{:S(2)}) collective-permute-start(f32[3,3,1,1,1024]{4,3,2,1,0:T(1,128)S(1)} %pad_maximum_fusion.3), channel_id=1, source_target_pairs={{0,1},{1,2},{2,3},{3,0},{4,5},{5,6},{6,7},{7,4},{8,9},{9,10},{10,1... | collective-permute-start | bytes 110600 | tf_op jit(solution)/shard_map/ppermute | solution.py:15
